TPU v7x, 32 devices: a whole 2x2x4 slice. The times are simulated.
32 devices in a mesh: expert: 4 (over y, x), dp: 8 (over z, core).
Axes of the slice: x: 2, y: 2, z: 4, core: 2. Of those that a mesh axis runs over, the one named last changes fastest.
Arguments:
- tokens: bfloat16 [2, 4096, 1280], P(None, ('expert', 'dp')), may hold values from -6 to 6
- modality: int32 [2, 4096], P(None, ('expert', 'dp')), may hold values from 0 to 1, as said below
- routes: int32 [2, 4096, 1], P(None, ('expert', 'dp')), may hold values from 0 to 3; in each aligned block of 128 rows (0 to 127, 128 to 255, ..., all dimensions but the last counted through in order) at most 64 rows name the same one
- router: bfloat16 [1280, 4], replicated, may hold values from -0.15625 to 0.15625
- w_in: bfloat16 [4, 1280, 5120], P('expert', 'dp'), may hold values from -0.15625 to 0.15625
- w_out: bfloat16 [4, 5120, 1280], P('expert', 'dp'), may hold values from -0.078125 to 0.078125
Outputs:
- mixed: bfloat16 [2, 4096, 1280], P(None, ('expert', 'dp'))
- load: float32 [2, 2, 4], replicated
Inputs may be any that keep to these rules, and one draw needn't show every extreme that they name: `routes`: among the 128 tokens of one micro-batch on one device (aligned blocks of 128 rows), at most 64 are routed to any one expert. `modality`: in every aligned block of 128 tokens of a micro-batch, the number of text tokens lies between 32 and 96.
All inputs are finite; a program needn't handle non-finite values.
Results may differ from a plain program's by a relative error of at most 0.0057.
Values may be sent and summed in bfloat16 or wider, within the bound.
A program may use at most 192 MiB of HBM per device.

v0:
```python
import functools

import jax
import jax.numpy as jnp
from jax import lax
from jax.experimental import pallas as pl
from jax.experimental.pallas import tpu as pltpu
from jax.sharding import PartitionSpec as P

MESH = pl.DeviceIdType.MESH


def layer_kernel(
    experts,
    ranks,
    tokens_ref,
    slots_ref,
    gating_ref,
    sums_ref,
    w_in_ref,
    w_out_ref,
    mixed_ref,
    total_ref,
    tok_far,
    slots_far,
    stats,
    win,
    wout,
    xs,
    xr,
    acc,
    hid,
    ys,
    yr,
    zs,
    zr,
    stat_sem,
    tok_sem,
    slot_sem,
    in_sem,
    out_sem,
    x_sem,
    y_sem,
    z_sem,
):
    micro, tok, width = tokens_ref.shape
    in_rows, ff = w_in_ref.shape
    out_rows = w_out_ref.shape[0]
    half_ff = ff // 2
    pieces, tile_w = zs.shape[0], zs.shape[3]
    cap = xs.shape[3]
    slots_all = experts * cap
    e = lax.axis_index("expert")
    p = lax.axis_index("dp")
    z, c = p // 2, p % 2
    chips = ranks // 2
    group = chips // 2
    h = z // group
    zl = z % group
    partner = ((z + group) % chips) * 2 + c
    mate = z * 2 + (1 - c)
    me = e * ranks + p
    total = experts * ranks

    barrier = pltpu.get_barrier_semaphore()

    def greet(k, carry):
        t = (me + k) % total
        pl.semaphore_signal(
            barrier, inc=1, device_id=(t // ranks, t % ranks), device_id_type=MESH
        )
        return carry

    lax.fori_loop(1, total, greet, 0)

    def remote(src, dst, sems, at, dp=None, expert=None):
        return pltpu.make_async_remote_copy(
            src_ref=src,
            dst_ref=dst,
            send_sem=sems.at[(0,) + at],
            recv_sem=sems.at[(1,) + at],
            device_id=(e if expert is None else expert, p if dp is None else dp),
            device_id_type=MESH,
        )

    def win_rows(q):
        return win.at[pl.ds(pl.multiple_of(q * in_rows, 16), in_rows), :]

    def wout_rows(q, piece):
        return wout.at[
            pl.ds(pl.multiple_of(q * out_rows, 16), out_rows), pl.ds(piece * tile_w, tile_w)
        ]

    def cols(which):
        return w_in_ref.at[:, pl.ds(pl.multiple_of(which * half_ff, 128), half_ff)]

    def peer(k):
        return (h * group + (zl + k) % group) * 2 + c

    def place(k):
        return ((zl + k) % group) * 2 + c

    pl.semaphore_wait(barrier, total - 1)

    pending = []

    def go(copy):
        copy.start()
        pending.append(copy)
        return copy

    tok_copy = go(remote(tokens_ref, tok_far, tok_sem, (), dp=partner))
    slot_copy = go(remote(slots_ref, slots_far, slot_sem, (), dp=partner))
    far_copy = go(remote(cols(1 - h), win_rows(p), in_sem, (1, 0, 0), dp=partner))
    near_copies = [
        go(remote(cols(h), win_rows(p), in_sem, (0, 0, k), dp=peer(k))) for k in range(1, group)
    ]
    near_mate = [go(remote(cols(h), win_rows(p), in_sem, (0, 1, 0), dp=mate))]
    own_in = pltpu.make_async_copy(cols(h), win_rows(p), in_sem.at[0, 0, 0, 0])
    own_in.start()

    def send_out(piece):
        src = w_out_ref.at[:, pl.ds(piece * tile_w, tile_w)]
        dst = wout_rows(place(0), piece)
        peers = [
            go(remote(src, dst, out_sem, (piece, 0, k), dp=peer(k))) for k in range(1, group)
        ]
        mates = [go(remote(src, dst, out_sem, (piece, 1, 0), dp=mate))]
        own = pltpu.make_async_copy(src, dst, out_sem.at[0, piece, 0, 0])
        own.start()
        return peers, mates, own

    early = pieces // 2
    out_sent = [send_out(piece) for piece in range(early)]

    def tell(k, carry):
        t = (me + k) % total
        pltpu.make_async_remote_copy(
            src_ref=sums_ref,
            dst_ref=stats.at[me],
            send_sem=stat_sem.at[0],
            recv_sem=stat_sem.at[1],
            device_id=(t // ranks, t % ranks),
            device_id_type=MESH,
        ).start()
        return carry

    lax.fori_loop(1, total, tell, 0)

    def placer_of(ref, m):
        hot = lax.broadcasted_iota(jnp.int32, (slots_all, tok), 0) == ref[m, 0:1, :]
        return jnp.where(hot, 1.0, 0.0).astype(jnp.bfloat16)

    def dispatch(side, tok_ref, slot_ref):
        for m in range(micro):
            put = jnp.dot(
                placer_of(slot_ref, m), tok_ref[m], preferred_element_type=jnp.float32
            ).astype(jnp.bfloat16)
            for to in range(experts):
                xs[side, to, m] = put[to * cap : (to + 1) * cap]
        copies = [
            go(
                remote(
                    xs.at[side, (e + k) % experts],
                    xr.at[side, e],
                    x_sem,
                    (side, k),
                    expert=(e + k) % experts,
                )
            )
            for k in range(1, experts)
        ]
        own = pltpu.make_async_copy(xs.at[side, e], xr.at[side, e], x_sem.at[0, side, 0])
        own.start()
        return copies, own

    def landed(copies, own):
        for copy in copies:
            copy.wait_recv()
        own.wait()

    own_x = dispatch(0, tokens_ref, slots_ref)
    tok_copy.wait_recv()
    slot_copy.wait_recv()
    far_x = dispatch(1, tok_far, slots_far)

    for k, copy in zip(range(1, group), near_copies):
        copy.wait_recv()
        rows = win_rows(peer(group - k))
        near_mate.append(go(remote(rows, rows, in_sem, (0, 1, k), dp=mate)))

    landed(*own_x)
    landed(*far_x)
    own_in.wait()
    for copy in near_mate:
        copy.wait_recv()

    side_rows = experts * micro * cap
    tile = 512 if half_ff % 512 == 0 else 128
    half_w = width // 2

    def first_dot(side, which, at):
        left = xr[side, :, :, :, pl.ds(pl.multiple_of(which * half_w, 128), half_w)]
        right = win[pl.ds(pl.multiple_of(which * half_w, 16), half_w), pl.ds(at, tile)]
        return jnp.dot(
            left.reshape(side_rows, half_w), right, preferred_element_type=jnp.float32
        )

    def near_tile(i, carry):
        at = pl.multiple_of(i * tile, 128)
        for side in range(2):
            acc[side, :, pl.ds(at, tile)] = first_dot(side, h, at)
        return carry

    far_copy.wait_recv()
    rows = win_rows(partner)
    far_copies = [
        go(remote(rows, rows, in_sem, (1, 0, k), dp=peer(k))) for k in range(1, group)
    ]
    far_mate = [go(remote(rows, rows, in_sem, (1, 1, 0), dp=mate))]
    out_sent += [send_out(piece) for piece in range(early, pieces)]

    lax.fori_loop(0, half_ff // tile, near_tile, 0)

    for k, copy in zip(range(1, group), far_copies):
        copy.wait_recv()
        source = (((z + group) % chips) // group) * group + (zl + group - k) % group
        rows = win_rows(source * 2 + c)
        far_mate.append(go(remote(rows, rows, in_sem, (1, 1, k), dp=mate)))
    for copy in far_mate:
        copy.wait_recv()

    def far_tile(i, carry):
        at = pl.multiple_of(i * tile, 128)
        for side in range(2):
            pre = acc[side, :, pl.ds(at, tile)] + first_dot(side, 1 - h, at)
            hid[side, :, pl.ds(at, tile)] = jax.nn.gelu(pre, approximate=True).astype(
                jnp.bfloat16
            )
        return carry

    lax.fori_loop(0, half_ff // tile, far_tile, 0)

    def second(side, piece):
        at = piece * tile_w
        got = jnp.dot(
            hid[side], wout[:, at : at + tile_w], preferred_element_type=jnp.float32
        ).astype(jnp.bfloat16)
        ys[side, piece] = got.reshape(experts, micro, cap, tile_w)
        copies = [
            go(
                remote(
                    ys.at[side, piece, (e + k) % experts],
                    yr.at[side, piece, e],
                    y_sem,
                    (side, piece, k),
                    expert=(e + k) % experts,
                )
            )
            for k in range(1, experts)
        ]
        own = pltpu.make_async_copy(
            ys.at[side, piece, e], yr.at[side, piece, e], y_sem.at[0, side, piece, 0]
        )
        own.start()
        return copies, own

    def combine(side, piece, m, slot_ref):
        back = yr[side, piece, :, m].reshape(slots_all, tile_w)
        return lax.dot_general(
            placer_of(slot_ref, m),
            back,
            (((0,), (0,)), ((), ())),
            preferred_element_type=jnp.float32,
        )

    far_y, own_y, z_copies = [], [], []

    def give_back(piece):
        landed(*far_y[piece])
        for m in range(micro):
            zs[piece, m] = combine(1, piece, m, slots_far).astype(jnp.bfloat16)
        z_copies.append(go(remote(zs.at[piece], zr.at[piece], z_sem, (piece,), dp=partner)))

    for piece, (peers, mates, own) in enumerate(out_sent):
        for k, copy in zip(range(1, group), peers):
            copy.wait_recv()
            rows = wout_rows(place(group - k), piece)
            mates.append(go(remote(rows, rows, out_sem, (piece, 1, k), dp=mate)))
        own.wait()
        for copy in mates:
            copy.wait_recv()
        far_y.append(second(1, piece))
        own_y.append(second(0, piece))
        if piece > 0:
            give_back(piece - 1)
    give_back(pieces - 1)

    everyone = stats.at[pl.ds(1, total - 1)]
    pltpu.make_async_copy(everyone, everyone, stat_sem.at[1]).wait()
    pltpu.make_async_copy(everyone, everyone, stat_sem.at[0]).wait()
    stats[me] = sums_ref[...]
    total_ref[...] = jnp.sum(stats[...], axis=0)

    for piece in range(pieces):
        landed(*own_y[piece])
        mine = [combine(0, piece, m, slots_ref) for m in range(micro)]
        z_copies[piece].wait_recv()
        for m in range(micro):
            both = mine[m] + zr[piece, m].astype(jnp.float32)
            mixed_ref[m, :, piece * tile_w : (piece + 1) * tile_w] = (
                both * gating_ref[m]
            ).astype(jnp.bfloat16)
    for copy in pending:
        copy.wait_send()


def on_device(tokens, modality, routes, router, w_in, w_out):
    micro, tok, width = tokens.shape
    experts = router.shape[1]
    cap = 2 * tok // experts
    ranks = lax.axis_size("dp")
    group = ranks // 4
    total = experts * ranks
    half_ff = w_in.shape[2] // 2
    tile_w = 256 if width % 256 == 0 else 128
    pieces = width // tile_w

    logits = jnp.einsum("mtd,de->mte", tokens, router, preferred_element_type=jnp.float32)
    onehot = (routes == jnp.arange(experts, dtype=jnp.int32)[None, None, :]).astype(jnp.float32)
    gating = jax.nn.sigmoid(jnp.sum(logits * onehot, axis=-1, keepdims=True))
    before = jnp.cumsum(onehot, axis=1) - 1.0
    slots = jnp.sum(before * onehot, axis=-1).astype(jnp.int32) + routes[:, :, 0] * cap
    slots = jnp.broadcast_to(slots[:, None, :], (micro, 8, tok))
    exps = jnp.exp(logits)
    router_probs = exps / jnp.sum(exps, axis=-1, keepdims=True)
    modal_hot = (modality[:, :, None] == jnp.arange(2, dtype=jnp.int32)[None, None, :]).astype(
        jnp.float32
    )
    columns = jnp.concatenate([onehot, router_probs, jnp.ones_like(gating)], axis=-1)
    sums = jnp.einsum("mtk,mtc->kc", modal_hot, columns, precision=lax.Precision.HIGHEST)
    sums = jnp.pad(sums, ((0, 6), (0, 128 - sums.shape[1])))

    bf16 = jnp.bfloat16
    dma = pltpu.SemaphoreType.DMA
    vmem = pl.BlockSpec(memory_space=pltpu.VMEM)
    mixed, summed = pl.pallas_call(
        functools.partial(layer_kernel, experts, ranks),
        out_shape=(
            jax.ShapeDtypeStruct(tokens.shape, bf16),
            jax.ShapeDtypeStruct((8, 128), jnp.float32),
        ),
        in_specs=[vmem] * 6,
        out_specs=(vmem, vmem),
        scratch_shapes=[
            pltpu.VMEM((micro, tok, width), bf16),
            pltpu.VMEM((micro, 8, tok), jnp.int32),
            pltpu.VMEM((total, 8, 128), jnp.float32),
            pltpu.VMEM((width, half_ff), bf16),
            pltpu.VMEM((half_ff, width), bf16),
            pltpu.VMEM((2, experts, micro, cap, width), bf16),
            pltpu.VMEM((2, experts, micro, cap, width), bf16),
            pltpu.VMEM((2, experts * micro * cap, half_ff), jnp.float32),
            pltpu.VMEM((2, experts * micro * cap, half_ff), bf16),
            pltpu.VMEM((2, pieces, experts, micro, cap, tile_w), bf16),
            pltpu.VMEM((2, pieces, experts, micro, cap, tile_w), bf16),
            pltpu.VMEM((pieces, micro, tok, tile_w), bf16),
            pltpu.VMEM((pieces, micro, tok, tile_w), bf16),
            dma((2,)),
            dma((2,)),
            dma((2,)),
            dma((2, 2, 2, group)),
            dma((2, pieces, 2, group)),
            dma((2, 2, experts)),
            dma((2, 2, pieces, experts)),
            dma((2, pieces)),
        ],
        compiler_params=pltpu.CompilerParams(
            collective_id=0, has_side_effects=True, vmem_limit_bytes=64 * 1024 * 1024 - 65536
        ),
    )(tokens, slots, gating, sums, w_in[0], w_out[0])

    counts, prob_sums = summed[:2, :experts], summed[:2, experts : 2 * experts]
    modal_counts = summed[:2, 2 * experts : 2 * experts + 1]
    load = jnp.stack([experts * counts / modal_counts, experts * prob_sums / modal_counts])
    return (mixed, load)


def solution(mesh):
    placed = (
        P(None, ("expert", "dp"), None),
        P(None, ("expert", "dp")),
        P(None, ("expert", "dp"), None),
        P(),
        P("expert", "dp", None),
        P("expert", "dp", None),
    )
    return jax.shard_map(
        on_device,
        mesh=mesh,
        in_specs=placed,
        out_specs=(P(None, ("expert", "dp"), None), P()),
        check_vma=False,
    )
```

profile of v0, /device:TPU:0, one launch (start us, length us, event | category | flops | bytes accessed | tf_op | source)
XLA Modules:
  0.0 156.6 jit_solution(6583702395017562965)
XLA Ops:
  0.6 0.7 fusion.7
  1.3 0.1 copy.10
  1.5 0.2 reduce_window_sum.11
  1.6 0.1 copy.11
  1.7 1.5 exponential_reduce_fusion
  3.2 0.1 pad.9.clone
  3.3 0.9 convolution_bitcast_fusion
  4.1 0.6 pad.4.sums_ref
  4.8 0.7 multiply_add_fusion
  5.4 0.6 broadcast_in_dim.2.slots_ref
  6.0 0.8 copy.12.gating_ref
  6.8 145.6 %shard_map.77 = (bf16[2,128,1280]{2,1,0:T(8,128)(2,1)}, f32[8,128]{1,0:T(8,128)}) custom-call(bf16[2,128,1280]{2,1,0:T(8,128)(2,1)} %tokens_ref.1, s32[2,8,128]{2,1,0:T(8,128)} %broadcast_in_dim.2.slots_ref, f32[2,128,1]{2,1,0:T(8,128)} %copy.12.gating_ref, f32[8,128]{1,0:T(8,128)} %pad.4.sums_ref, bf16[160,5120]{1,0:T(8,128)(2,1)} %bitcast.18, ...), custom_call_target="tpu_custom_call" | custom-call | tf_op jit(solution)/shard_map/pallas_call | solution.py:347
  152.4 0.9 slice_reduce_fusion
  153.3 0.8 divide_bitcast_fusion.1
  154.1 0.6 pad_maximum_fusion
  154.7 2.0 %copy.14 = bf16[2,128,1280]{2,1,0:T(8,128)(2,1)} copy(bf16[2,128,1280]{2,1,0:T(8,128)(2,1)} %get-tuple-element.14) | data formatting | bytes 1310720
  (2 shorter events, 0.0 us)
where the time goes:
time: 157 us
  Pallas kernels  146 us (93%)
  local copies, waits for them, and re-layouts  5.11 us (3%)
  other arithmetic  2.98 us (2%)
  matrix products  2.32 us (1%)
    pallas_call x1, Pallas kernels, on_device(): pl.pallas_call(functools.partial(layer_kernel, experts, ranks), out_shape...  146 us

commit v1 on v0

v1 whole, which is shorter than its diff:
```python
import functools

import jax
import jax.numpy as jnp
from jax import lax
from jax.experimental import pallas as pl
from jax.experimental.pallas import tpu as pltpu
from jax.sharding import PartitionSpec as P

MESH = pl.DeviceIdType.MESH
BF16 = jnp.bfloat16
F32 = jnp.float32


def layer_kernel(
    experts,
    ranks,
    splits,
    tokens_ref,
    routes_ref,
    modality_ref,
    router_ref,
    w_in_ref,
    w_out_ref,
    mixed_ref,
    load_ref,
    tok_far,
    routes_far,
    slot_row,
    back_hot,
    gate,
    sums,
    stats_e,
    stats_d,
    win,
    wout,
    xs,
    xr,
    acc,
    hid,
    ys,
    yr,
    zs,
    zr,
    tok_sem,
    routes_sem,
    stat_sem,
    far_sem,
    in_send,
    in_recv,
    out_send,
    out_recv,
    x_sem,
    x_own,
    y_sem,
    y_own,
    z_send,
    z_recv,
):
    micro, tok, width = tokens_ref.shape
    in_rows, ff = w_in_ref.shape
    out_rows = w_out_ref.shape[0]
    half_ff = ff // 2
    pieces, tile_w = zr.shape[0], zr.shape[3]
    cap = xs.shape[3]
    slots_all = experts * cap
    side_rows = experts * micro * cap
    e = lax.axis_index("expert")
    p = lax.axis_index("dp")
    z, c = p // 2, p % 2
    chips = ranks // 2
    group = chips // 2
    pairs = group // 2
    h = z // group
    zl = z % group
    mate = z * 2 + (1 - c)
    inner = (z % 2) == (1 - h)
    outer = (z % 2) == h
    role = (z + h) % 2

    def far_rank(t, which, core):
        pair = (1 - h) * pairs + ((z // 2) % pairs + t) % pairs
        return (pair * 2 + (1 - h + which) % 2) * 2 + core

    far_in = far_rank(0, 1, c)
    far_out = far_rank(0, 0, c)

    def peer(k):
        return (h * group + (zl + k) % group) * 2 + c

    def place(k, core):
        return ((zl + k) % group) * 2 + core

    barrier = pltpu.get_barrier_semaphore()

    def greet_e(k, carry):
        pl.semaphore_signal(
            barrier, inc=1, device_id=((e + k) % experts, p), device_id_type=MESH
        )
        return carry

    def greet_d(k, carry):
        pl.semaphore_signal(barrier, inc=1, device_id=(e, (p + k) % ranks), device_id_type=MESH)
        return carry

    lax.fori_loop(1, experts, greet_e, 0)
    lax.fori_loop(1, ranks, greet_d, 0)

    def remote(src, dst, send, recv, dp=None, expert=None):
        return pltpu.make_async_remote_copy(
            src_ref=src,
            dst_ref=dst,
            send_sem=send,
            recv_sem=recv,
            device_id=(e if expert is None else expert, p if dp is None else dp),
            device_id_type=MESH,
        )

    def arrive(ref, sem):
        pltpu.make_async_copy(ref, ref, sem).wait()

    def win_rows(q, start=0, size=half_ff):
        return win.at[pl.ds(pl.multiple_of(q * in_rows, 16), in_rows), pl.ds(start, size)]

    def wout_rows(r, piece):
        return wout.at[
            pl.ds(pl.multiple_of(r * out_rows, 16), out_rows), pl.ds(piece * tile_w, tile_w)
        ]

    def cols(which, start=0, size=half_ff):
        return w_in_ref.at[:, pl.ds(pl.multiple_of(which * half_ff + start, 128), size)]

    def w_out_piece(piece):
        return w_out_ref.at[:, pl.ds(piece * tile_w, tile_w)]

    tok_copy = remote(
        tokens_ref, tok_far.at[role], tok_sem.at[0, 0], tok_sem.at[1, role], dp=far_in
    )
    routes_copy = remote(
        routes_ref, routes_far.at[role], routes_sem.at[0, 0], routes_sem.at[1, role], dp=far_in
    )
    far_copies = [
        remote(cols(1 - h, at, size), win_rows(p, at, size), far_sem.at[j], in_recv.at[p, j], dp=far_in)
        for j, (at, size) in enumerate(splits)
    ]
    near_peers = [
        remote(cols(h), win_rows(p), in_send.at[p, 0, k], in_recv.at[p, 0], dp=peer(k))
        for k in range(1, group)
    ]
    near_mate = remote(cols(h), win_rows(p), in_send.at[p, 0, 0], in_recv.at[p, 0], dp=mate)
    own_in = pltpu.make_async_copy(cols(h), win_rows(p), in_recv.at[p, 0])
    mine = place(0, c)
    out_peers = [
        [
            remote(
                w_out_piece(i), wout_rows(mine, i), out_send.at[mine, i, k], out_recv.at[mine, i],
                dp=peer(k),
            )
            for k in range(1, group)
        ]
        for i in range(pieces)
    ]
    out_mate = [
        remote(
            w_out_piece(i), wout_rows(mine, i), out_send.at[mine, i, 0], out_recv.at[mine, i], dp=mate
        )
        for i in range(pieces)
    ]
    own_out = [
        pltpu.make_async_copy(w_out_piece(i), wout_rows(mine, i), out_recv.at[mine, i])
        for i in range(pieces)
    ]

    def pass_near(k):
        q = peer(k)
        return remote(win_rows(q), win_rows(q), in_send.at[q, 0, 0], in_recv.at[q, 0], dp=mate)

    def pass_far(q, j, k):
        at, size = splits[j]
        rows = win_rows(q, at, size)
        to = mate if k == 0 else peer(k)
        return remote(rows, rows, in_send.at[q, j, k], in_recv.at[q, j], dp=to)

    def pass_out(k, i):
        r = place(k, c)
        rows = wout_rows(r, i)
        return remote(rows, rows, out_send.at[r, i, 0], out_recv.at[r, i], dp=mate)

    pl.semaphore_wait(barrier, experts + ranks - 2)

    early = pieces - 2
    routes_copy.start()
    tok_copy.start()

    @pl.when(inner)
    def _():
        for copy in far_copies:
            copy.start()
        for copy in near_peers:
            copy.start()
        for i in range(early):
            for copy in out_peers[i]:
                copy.start()

    @pl.when(outer)
    def _():
        for copy in near_peers:
            copy.start()
        for copy in far_copies:
            copy.start()
        for i in range(pieces):
            for copy in out_peers[i]:
                copy.start()

    near_mate.start()
    own_in.start()
    for i in range(pieces):
        out_mate[i].start()
        own_out[i].start()

    rows_e = max(experts, 8)

    def hot_of(row):
        at = lax.broadcasted_iota(jnp.int32, (rows_e, tok), 0)
        return jnp.where(at == row, 1.0, 0.0)

    def spread(row):
        return jnp.broadcast_to(row, (tok, tok)).T

    def assign(side, ref):
        ahead = lax.broadcasted_iota(jnp.int32, (tok, tok), 0) < lax.broadcasted_iota(
            jnp.int32, (tok, tok), 1
        )
        ahead = jnp.where(ahead, 1.0, 0.0).astype(BF16)
        for m in range(micro):
            row = ref[m : m + 1, :]
            hot = hot_of(row)
            before = jnp.dot(hot.astype(BF16), ahead, preferred_element_type=F32)
            slot = jnp.sum(hot * before, axis=0, keepdims=True) + row.astype(F32) * cap
            slot_row[side, m] = jnp.broadcast_to(slot, (8, tok))

    def assign_back(side):
        lanes = lax.broadcasted_iota(jnp.int32, (tok, slots_all), 1).astype(F32)
        for m in range(micro):
            slot = spread(slot_row[side, m, 0:1, :])
            wide = jnp.concatenate([slot] * (slots_all // tok), axis=1)
            back_hot[side, m] = jnp.where(lanes == wide, 1.0, 0.0).astype(BF16)

    def x_copy(side, to):
        return remote(
            xs.at[side, to], xr.at[side, e], x_sem.at[0, side], x_sem.at[1, side], expert=to
        )

    def x_keep(side):
        return pltpu.make_async_copy(xs.at[side, e], xr.at[side, e], x_own.at[side])

    def dispatch(side, tok_ref):
        for m in range(micro):
            hot = lax.broadcasted_iota(jnp.int32, (slots_all, tok), 0).astype(F32)
            hot = jnp.where(hot == slot_row[side, m, 0:1, :], 1.0, 0.0).astype(BF16)
            put = jnp.dot(hot, tok_ref[m], preferred_element_type=F32).astype(BF16)
            for to in range(experts):
                xs[side, to, m] = put[to * cap : (to + 1) * cap]
        for k in range(1, experts):
            x_copy(side, (e + k) % experts).start()
        x_keep(side).start()

    def x_landed(side):
        arrive(xr.at[side, pl.ds(1, experts - 1)], x_sem.at[1, side])
        x_keep(side).wait()

    assign(0, routes_ref)
    dispatch(0, tokens_ref)

    counted = jnp.zeros((8, experts), F32)
    summed = jnp.zeros((8, experts), F32)
    present = jnp.zeros((8, 1), F32)
    for m in range(micro):
        logits = lax.dot_general(
            router_ref[...], tokens_ref[m], (((1,), (1,)), ((), ())), preferred_element_type=F32
        )
        row = routes_ref[m : m + 1, :]
        hot = jnp.where(lax.broadcasted_iota(jnp.int32, (experts, tok), 0) == row, 1.0, 0.0)
        chosen = jnp.sum(logits * hot, axis=0, keepdims=True)
        gate[m] = spread(1.0 / (1.0 + jnp.exp(-chosen)))
        exps = jnp.exp(logits)
        probs = exps / jnp.sum(exps, axis=0, keepdims=True)
        modal = lax.broadcasted_iota(jnp.int32, (8, tok), 0) == modality_ref[m : m + 1, :]
        modal = jnp.where(modal, 1.0, 0.0)
        counted += lax.dot_general(
            modal, hot, (((1,), (1,)), ((), ())),
            precision=lax.Precision.HIGHEST, preferred_element_type=F32,
        )
        summed += lax.dot_general(
            modal, probs, (((1,), (1,)), ((), ())),
            precision=lax.Precision.HIGHEST, preferred_element_type=F32,
        )
        present += jnp.sum(modal, axis=1, keepdims=True)
    sums[0] = jnp.zeros((8, 128), F32)
    sums[0, 0:2, 0:experts] = counted[0:2]
    sums[0, 2:4, 0:experts] = summed[0:2]
    sums[0, 4:6, 0:experts] = jnp.broadcast_to(present[0:2], (2, experts))

    def tell_e(k, carry):
        remote(
            sums.at[0], stats_e.at[e], stat_sem.at[0, 0], stat_sem.at[1, 0], expert=(e + k) % experts
        ).start()
        return carry

    def tell_d(k, carry):
        remote(
            sums.at[1], stats_d.at[p], stat_sem.at[0, 1], stat_sem.at[1, 1], dp=(p + k) % ranks
        ).start()
        return carry

    lax.fori_loop(1, experts, tell_e, 0)
    assign_back(0)

    def second_stats():
        arrive(stats_e.at[pl.ds(1, experts - 1)], stat_sem.at[1, 0])
        stats_e[e] = sums[0]
        sums[1] = jnp.sum(stats_e[...], axis=0)
        lax.fori_loop(1, ranks, tell_d, 0)

    tile = 512 if half_ff % 512 == 0 else 128
    half_w = width // 2

    def first_dot(side, which, at):
        left = xr[side, :, :, :, pl.ds(pl.multiple_of(which * half_w, 128), half_w)]
        right = win[pl.ds(pl.multiple_of(which * half_w, 16), half_w), pl.ds(at, tile)]
        return jnp.dot(left.reshape(side_rows, half_w), right, preferred_element_type=F32)

    def near_side(side):
        def near_tile(i, carry):
            at = pl.multiple_of(i * tile, 128)
            acc[side, :, pl.ds(at, tile)] = first_dot(side, h, at)
            return carry

        lax.fori_loop(0, half_ff // tile, near_tile, 0)

    def far_sides(sides, j):
        start, size = splits[j]
        count = size // tile

        def far_tile(i, carry):
            side = i % sides
            at = pl.multiple_of(start + (i // sides) * tile, 128)
            pre = acc[side, :, pl.ds(at, tile)] + first_dot(side, 1 - h, at)
            hid[side, :, pl.ds(at, tile)] = jax.nn.gelu(pre, approximate=True).astype(BF16)
            return carry

        lax.fori_loop(0, count * sides, far_tile, 0)

    def near_arrived():
        for k in range(1, group):
            arrive(win_rows(peer(k)), in_recv.at[peer(k), 0])
            pass_near(k).start()

    def near_whole():
        own_in.wait()
        for k in range(group):
            q = (h * group + (zl + k) % group) * 2 + (1 - c)
            arrive(win_rows(q), in_recv.at[q, 0])

    def far_arrived(t, which, j):
        q = far_rank(t, which, c)
        arrive(win_rows(q, *splits[j]), in_recv.at[q, j])
        pass_far(q, j, 0).start()

    def far_direct(which, j):
        q = far_rank(0, which, c)
        arrive(win_rows(q, *splits[j]), in_recv.at[q, j])
        for k in range(1, group):
            pass_far(q, j, k).start()
        pass_far(q, j, 0).start()

    def far_whole(j):
        for t in range(pairs):
            for which in range(2):
                q = far_rank(t, which, 1 - c)
                arrive(win_rows(q, *splits[j]), in_recv.at[q, j])

    def out_arrived(i):
        for k in range(1, group):
            r = place(k, c)
            arrive(wout_rows(r, i), out_recv.at[r, i])
            pass_out(k, i).start()

    def out_whole(i):
        own_out[i].wait()
        for k in range(group):
            r = place(k, 1 - c)
            arrive(wout_rows(r, i), out_recv.at[r, i])

    def second(side, i):
        got = jnp.dot(
            hid[side], wout[:, i * tile_w : (i + 1) * tile_w], preferred_element_type=F32
        ).astype(BF16)
        ys[side, i] = got.reshape(experts, micro, cap, tile_w)

    def y_keep(side, i):
        return pltpu.make_async_copy(ys.at[side, i, e], yr.at[side, i, e], y_own.at[side, i])

    def y_start(side, i):
        for k in range(1, experts):
            to = (e + k) % experts
            remote(
                ys.at[side, i, to], yr.at[side, i, e], y_sem.at[0, side, i], y_sem.at[1, side, i],
                expert=to,
            ).start()
        y_keep(side, i).start()

    def y_landed(side, i):
        arrive(yr.at[side, i, pl.ds(1, experts - 1)], y_sem.at[1, side, i])
        y_keep(side, i).wait()

    def combine(side, i, m):
        back = yr[side, i, :, m].reshape(slots_all, tile_w)
        return jnp.dot(back_hot[side, m], back, preferred_element_type=F32)

    def z_copy(side, i):
        return remote(
            zs.at[side - 1, i], zr.at[i], z_send.at[side - 1, i], z_recv.at[i],
            dp=far_out if side == 1 else far_in,
        )

    def give_back(side, i):
        y_landed(side, i)
        for m in range(micro):
            zs[side - 1, i, m] = combine(side, i, m).astype(BF16)
        z_copy(side, i).start()

    last = len(splits) - 1

    @pl.when(inner)
    def _():
        for which in range(2):
            arrive(routes_far.at[which], routes_sem.at[1, which])
            arrive(tok_far.at[which], tok_sem.at[1, which])
            assign(1 + which, routes_far.at[which])
            dispatch(1 + which, tok_far.at[which])
            assign_back(1 + which)
        second_stats()
        near_arrived()
        x_landed(0)
        near_whole()
        near_side(0)
        x_landed(1)
        near_side(1)
        x_landed(2)
        near_side(2)
        for j in range(last + 1):
            far_direct(0, j)
        for copy in out_peers[early]:
            copy.start()
        for j in range(last + 1):
            far_direct(1, j)
            for t in range(1, pairs):
                far_arrived(t, 0, j)
                far_arrived(t, 1, j)
            if j == last:
                for i in range(early + 1, pieces):
                    for copy in out_peers[i]:
                        copy.start()
                out_arrived(0)
            far_whole(j)
            far_sides(3, j)
        for i in range(pieces):
            if i + 1 < pieces:
                out_arrived(i + 1)
            out_whole(i)
            for side in (2, 1):
                second(side, i)
                y_start(side, i)
            second(0, i)
            if i > 0:
                for side in (2, 1):
                    give_back(side, i - 1)
        for i in range(pieces):
            y_start(0, i)
        for side in (2, 1):
            give_back(side, pieces - 1)

    @pl.when(outer)
    def _():
        second_stats()
        near_arrived()
        x_landed(0)
        near_whole()
        near_side(0)
        for i in range(early):
            out_arrived(i)
        for j in range(last + 1):
            for t in range(pairs):
                far_arrived(t, 0, j)
                far_arrived(t, 1, j)
            far_whole(j)
            far_sides(1, j)
        for i in range(pieces):
            if i >= early:
                out_arrived(i)
            out_whole(i)
            second(0, i)
            y_start(0, i)

    arrive(stats_d.at[pl.ds(1, ranks - 1)], stat_sem.at[1, 1])
    stats_d[p] = sums[1]
    sums[2] = jnp.sum(stats_d[...], axis=0)
    modal_counts = sums[2, 4:6, 0:experts]
    load_ref[0] = experts * sums[2, 0:2, 0:experts] / modal_counts
    load_ref[1] = experts * sums[2, 2:4, 0:experts] / modal_counts

    for i in range(pieces):
        y_landed(0, i)
        kept = [combine(0, i, m) for m in range(micro)]
        arrive(zr.at[i], z_recv.at[i])
        for m in range(micro):
            both = kept[m] + zr[i, m].astype(F32)
            scale = jnp.concatenate([gate[m]] * (tile_w // tok), axis=1)
            mixed_ref[m, :, i * tile_w : (i + 1) * tile_w] = (both * scale).astype(BF16)

    arrive(stats_e.at[pl.ds(1, experts - 1)], stat_sem.at[0, 0])
    arrive(stats_d.at[pl.ds(1, ranks - 1)], stat_sem.at[0, 1])
    for copy in [tok_copy, routes_copy, near_mate] + far_copies + near_peers + out_mate:
        copy.wait_send()
    for i in range(pieces):
        for copy in out_peers[i]:
            copy.wait_send()
        for k in range(1, group):
            pass_out(k, i).wait_send()
    for k in range(1, group):
        pass_near(k).wait_send()
    for t in range(pairs):
        for which in range(2):
            for j in range(last + 1):
                pass_far(far_rank(t, which, c), j, 0).wait_send()

    def sent(side):
        arrive(xr.at[side, pl.ds(1, experts - 1)], x_sem.at[0, side])
        for i in range(pieces):
            arrive(yr.at[side, i, pl.ds(1, experts - 1)], y_sem.at[0, side, i])

    sent(0)

    @pl.when(inner)
    def _():
        for side in (1, 2):
            sent(side)
            for i in range(pieces):
                z_copy(side, i).wait_send()
        for which in range(2):
            for j in range(last + 1):
                for k in range(1, group):
                    pass_far(far_rank(0, which, c), j, k).wait_send()


def on_device(tokens, modality, routes, router, w_in, w_out):
    micro, tok, width = tokens.shape
    experts = router.shape[1]
    cap = 2 * tok // experts
    ranks = lax.axis_size("dp")
    group = ranks // 4
    half_ff = w_in.shape[2] // 2
    tile_w = 256 if width % 256 == 0 else 128
    pieces = width // tile_w
    tile = 512 if half_ff % 512 == 0 else 128
    first = (half_ff // tile + 1) // 2 * tile
    splits = ((0, first), (first, half_ff - first))
    parts = len(splits)

    dma = pltpu.SemaphoreType.DMA
    vmem = pl.BlockSpec(memory_space=pltpu.VMEM)
    hbm = pl.BlockSpec(memory_space=pl.ANY)
    rows = experts * micro * cap
    mixed, load = pl.pallas_call(
        functools.partial(layer_kernel, experts, ranks, splits),
        out_shape=(
            jax.ShapeDtypeStruct(tokens.shape, BF16),
            jax.ShapeDtypeStruct((2, 2, experts), F32),
        ),
        in_specs=[vmem] * 4 + [hbm] * 2,
        out_specs=(vmem, vmem),
        scratch_shapes=[
            pltpu.VMEM((2, micro, tok, width), BF16),
            pltpu.VMEM((2, micro, tok), jnp.int32),
            pltpu.VMEM((3, micro, 8, tok), F32),
            pltpu.VMEM((3, micro, tok, experts * cap), BF16),
            pltpu.VMEM((micro, tok, tok), F32),
            pltpu.VMEM((3, 8, 128), F32),
            pltpu.VMEM((experts, 8, 128), F32),
            pltpu.VMEM((ranks, 8, 128), F32),
            pltpu.VMEM((width, half_ff), BF16),
            pltpu.VMEM((half_ff, width), BF16),
            pltpu.VMEM((3, experts, micro, cap, width), BF16),
            pltpu.VMEM((3, experts, micro, cap, width), BF16),
            pltpu.VMEM((3, rows, half_ff), F32),
            pltpu.VMEM((3, rows, half_ff), BF16),
            pltpu.VMEM((3, pieces, experts, micro, cap, tile_w), BF16),
            pltpu.VMEM((3, pieces, experts, micro, cap, tile_w), BF16),
            pltpu.VMEM((2, pieces, micro, tok, tile_w), BF16),
            pltpu.VMEM((pieces, micro, tok, tile_w), BF16),
            dma((2, 2)),
            dma((2, 2)),
            dma((2, 2)),
            dma((parts,)),
            dma((ranks, parts, group)),
            dma((ranks, parts)),
            dma((2 * group, pieces, group)),
            dma((2 * group, pieces)),
            dma((2, 3)),
            dma((3,)),
            dma((2, 3, pieces)),
            dma((3, pieces)),
            dma((2, pieces)),
            dma((pieces,)),
        ],
        compiler_params=pltpu.CompilerParams(
            collective_id=0, has_side_effects=True, vmem_limit_bytes=64 * 1024 * 1024 - 65536
        ),
    )(tokens, routes[:, :, 0], modality, router.T, w_in[0], w_out[0])
    return (mixed, load)


def solution(mesh):
    placed = (
        P(None, ("expert", "dp"), None),
        P(None, ("expert", "dp")),
        P(None, ("expert", "dp"), None),
        P(),
        P("expert", "dp", None),
        P("expert", "dp", None),
    )
    return jax.shard_map(
        on_device,
        mesh=mesh,
        in_specs=placed,
        out_specs=(P(None, ("expert", "dp"), None), P()),
        check_vma=False,
    )
```

time: 157 us -> 135 us (0.86)
  Pallas kernels: 146 us -> 130 us
  other arithmetic: 2.98 us -> 0 us
  matrix products: 2.32 us -> 0 us
  local copies, waits for them, and re-layouts: 5.11 us -> 3.21 us
    pallas_call x1, Pallas kernels: 146 us -> 130 us  [on_device(): pl.pallas_call(functools.partial(layer_kernel, experts, ranks, splits), o...]
    dot_general x2 -> x0, matrix products: 2.32 us -> none  [the longest x1 1.45 us: on_device(): jnp.einsum('mtd,de->mte', tokens, router, preferred_element_type=jnp.floa...]
    another operation x3 -> x0, other arithmetic: 1.6 us -> none  [the longest x2 1.4 us: on_device(): jnp.stack([experts * counts / modal_counts, experts * prob_sums / modal_c...]
    unnamed x1 -> x2, local copies, waits for them, and re-layouts: 1.96 us -> 3.21 us
where the time goes in v1:
time: 135 us; the launch traced here: 134 us
  Pallas kernels  130 us (96%)
  local copies, waits for them, and re-layouts  3.21 us (2%)
    pallas_call x1, Pallas kernels, on_device(): pl.pallas_call(functools.partial(layer_kernel, experts, ranks, splits), o...  130 us
    unnamed x2, local copies, waits for them, and re-layouts  3.21 us

profile of v1, /device:TPU:0, one launch (start us, length us, event | category | flops | bytes accessed | tf_op | source)
XLA Modules:
  0.0 134.2 jit_solution(1806673637015931682)
XLA Ops:
  0.6 130.3 %shard_map.77 = (bf16[2,128,1280]{2,1,0:T(8,128)(2,1)}, f32[2,2,4]{2,1,0:T(2,128)}) custom-call(bf16[2,128,1280]{2,1,0:T(8,128)(2,1)} %tokens_ref.1, s32[2,128]{1,0:T(2,128)} %bitcast.7, s32[2,128]{1,0:T(2,128)} %modality_ref.1, bf16[4,1280]{1,0:T(4,128)(2,1)} %bitcast.6, bf16[160,5120]{1,0:T(8,128)(2,1)} %bitcast.4, bf16[640,1280]{1,0:T(8,128)(2,1)} %bitcast.5), custom_call_target="tpu_custom_call" | custom-call | tf_op jit(solution)/shard_map/pallas_call | solution.py:575
  131.0 2.0 %copy.10 = bf16[2,128,1280]{2,1,0:T(8,128)(2,1)} copy(bf16[2,128,1280]{2,1,0:T(8,128)(2,1)} %get-tuple-element.4) | data formatting | bytes 1310720
  133.0 1.2 copy.11

commit v2 on v1

v2 whole, which is shorter than its diff:
```python
import functools
import math

import jax
import jax.numpy as jnp
from jax import lax
from jax.experimental import pallas as pl
from jax.experimental.pallas import tpu as pltpu
from jax.sharding import PartitionSpec as P

MESH = pl.DeviceIdType.MESH
BF16 = jnp.bfloat16
F32 = jnp.float32
C1 = math.sqrt(2 / math.pi)
C3 = 0.044715 * C1


def layer_kernel(
    experts,
    ranks,
    tile,
    tokens_ref,
    routes_ref,
    modality_ref,
    router_ref,
    w_in_ref,
    w_out_ref,
    mixed_ref,
    load_ref,
    tok_own,
    result,
    tok_far,
    routes_far,
    slot_row,
    back_hot,
    gate,
    sums,
    stats_e,
    stats_d,
    win,
    wout,
    xs,
    xr,
    acc,
    hid,
    ys,
    yr,
    zs,
    zr,
    w_part,
    tok_sem,
    routes_sem,
    stat_sem,
    in_send,
    near_recv,
    near_whole_recv,
    far_recv,
    far_whole_recv,
    out_send,
    out_recv,
    out_whole_recv,
    x_sem,
    y_send,
    y_recv,
    z_send,
    z_recv,
    w_send,
    w_recv,
    load_sem,
    result_sem,
):
    micro, tok, width = tokens_ref.shape
    in_rows, ff = w_in_ref.shape
    out_rows = w_out_ref.shape[0]
    half_ff = ff // 2
    pieces, tile_w = zr.shape[0], zr.shape[3]
    direct = w_part.shape[0]
    cap = xs.shape[3]
    slots_all = experts * cap
    side_rows = experts * micro * cap
    e = lax.axis_index("expert")
    p = lax.axis_index("dp")
    z, c = p // 2, p % 2
    chips = ranks // 2
    group = chips // 2
    pairs = group // 2
    h = z // group
    zl = z % group
    mate = z * 2 + (1 - c)
    inner = (z % 2) == (1 - h)
    outer = (z % 2) == h
    role = (z + h) % 2

    def far_rank(t, which, core):
        pair = (1 - h) * pairs + ((z // 2) % pairs + t) % pairs
        return (pair * 2 + (1 - h + which) % 2) * 2 + core

    far_in = far_rank(0, 1, c)
    far_out = far_rank(0, 0, c)

    def peer(k):
        return (h * group + (zl + k) % group) * 2 + c

    def place(k, core):
        return ((zl + k) % group) * 2 + core

    tok_load = pltpu.make_async_copy(tokens_ref, tok_own, load_sem)
    tok_load.start()
    barrier = pltpu.get_barrier_semaphore()

    def greet_e(k, carry):
        pl.semaphore_signal(
            barrier, inc=1, device_id=((e + k) % experts, p), device_id_type=MESH
        )
        return carry

    def greet_d(k, carry):
        pl.semaphore_signal(barrier, inc=1, device_id=(e, (p + k) % ranks), device_id_type=MESH)
        return carry

    lax.fori_loop(1, experts, greet_e, 0)
    lax.fori_loop(1, ranks, greet_d, 0)

    def remote(src, dst, send, recv, dp=None, expert=None):
        return pltpu.make_async_remote_copy(
            src_ref=src,
            dst_ref=dst,
            send_sem=send,
            recv_sem=recv,
            device_id=(e if expert is None else expert, p if dp is None else dp),
            device_id_type=MESH,
        )

    def arrive(ref, sem):
        pltpu.make_async_copy(ref, ref, sem).wait()

    parts = half_ff // tile

    def chunk(j):
        return (j * tile if isinstance(j, int) else pl.multiple_of(j * tile, 128), tile)

    def win_rows(q, start=0, size=half_ff):
        return win.at[pl.ds(pl.multiple_of(q * in_rows, 16), in_rows), pl.ds(start, size)]

    def wout_rows(r, piece):
        return wout.at[
            pl.ds(pl.multiple_of(r * out_rows, 16), out_rows), pl.ds(piece * tile_w, tile_w)
        ]

    def cols(which, start=0, size=half_ff):
        return w_in_ref.at[:, pl.ds(pl.multiple_of(which * half_ff + start, 128), size)]

    def w_out_piece(piece):
        return w_out_ref.at[:, pl.ds(piece * tile_w, tile_w)]

    tok_copy = remote(
        tok_own, tok_far.at[role], tok_sem.at[2], tok_sem.at[role], dp=far_in
    )
    routes_copy = remote(
        routes_ref, routes_far.at[role], routes_sem.at[2], routes_sem.at[role], dp=far_in
    )
    far_copies = [
        remote(
            cols(1 - h, *chunk(j)), win_rows(p, *chunk(j)), in_send.at[0], far_recv.at[zl, j], dp=far_in
        )
        for j in range(parts)
    ]
    near_peers = [
        remote(cols(h), win_rows(p), in_send.at[0], near_recv.at[zl], dp=peer(k))
        for k in range(1, group)
    ]
    near_mate = remote(cols(h), win_rows(p), in_send.at[0], near_whole_recv, dp=mate)
    own_in = pltpu.make_async_copy(cols(h), win_rows(p), near_whole_recv)
    mine = place(0, c)
    out_peers = [
        [
            remote(
                w_out_piece(i), wout_rows(mine, i), out_send, out_recv.at[zl, i], dp=peer(k)
            )
            for k in range(1, group)
        ]
        for i in range(pieces)
    ]
    out_mate = [
        remote(
            w_out_piece(i), wout_rows(mine, i), out_send, out_whole_recv.at[i], dp=mate
        )
        for i in range(pieces)
    ]
    own_out = [
        pltpu.make_async_copy(w_out_piece(i), wout_rows(mine, i), out_whole_recv.at[i])
        for i in range(pieces)
    ]

    def pass_near(k):
        q = peer(k)
        return remote(win_rows(q), win_rows(q), in_send.at[0], near_whole_recv, dp=mate)

    def pass_far(q, j, k):
        rows = win_rows(q, *chunk(j))
        if k == 0:
            return remote(rows, rows, in_send.at[0], far_whole_recv.at[j], dp=mate)
        at = (q // 2) % group
        return remote(rows, rows, in_send.at[1], far_recv.at[at, j], dp=peer(k))

    def pass_out(k, i):
        r = place(k, c)
        rows = wout_rows(r, i)
        return remote(rows, rows, out_send, out_whole_recv.at[i], dp=mate)

    tok_load.wait()
    pl.semaphore_wait(barrier, experts + ranks - 2)

    early = pieces - 1
    routes_copy.start()
    tok_copy.start()

    @pl.when(inner)
    def _():
        for copy in far_copies:
            copy.start()
        for copy in near_peers:
            copy.start()
        for i in range(2):
            for copy in out_peers[i]:
                copy.start()

    @pl.when(outer)
    def _():
        for copy in far_copies[:2]:
            copy.start()
        for copy in near_peers:
            copy.start()
        for copy in far_copies[2:]:
            copy.start()
        for i in range(pieces):
            for copy in out_peers[i]:
                copy.start()


    rows_e = max(experts, 8)

    def hot_of(row):
        at = lax.broadcasted_iota(jnp.int32, (rows_e, tok), 0)
        return jnp.where(at == row, 1.0, 0.0)

    def spread(row):
        return jnp.broadcast_to(row, (tok, tok)).T

    def assign(side, ref):
        ahead = lax.broadcasted_iota(jnp.int32, (tok, tok), 0) < lax.broadcasted_iota(
            jnp.int32, (tok, tok), 1
        )
        ahead = jnp.where(ahead, 1.0, 0.0).astype(BF16)
        for m in range(micro):
            row = ref[m : m + 1, :]
            hot = hot_of(row)
            before = jnp.dot(hot.astype(BF16), ahead, preferred_element_type=F32)
            slot = jnp.sum(hot * before, axis=0, keepdims=True) + row.astype(F32) * cap
            slot_row[side, m] = jnp.broadcast_to(slot, (8, tok))

    def assign_back(side):
        lanes = lax.broadcasted_iota(jnp.int32, (tok, slots_all), 1).astype(F32)
        for m in range(micro):
            slot = spread(slot_row[side, m, 0:1, :])
            wide = jnp.concatenate([slot] * (slots_all // tok), axis=1)
            back_hot[side, m] = jnp.where(lanes == wide, 1.0, 0.0).astype(BF16)

    def x_copy(side, to):
        return remote(
            xs.at[side, to], xr.at[side, e], x_sem.at[0, side], x_sem.at[1, side], expert=to
        )

    def dispatch(side, tok_ref):
        for m in range(micro):
            hot = lax.broadcasted_iota(jnp.int32, (slots_all, tok), 0).astype(F32)
            hot = jnp.where(hot == slot_row[side, m, 0:1, :], 1.0, 0.0).astype(BF16)
            put = jnp.dot(hot, tok_ref[m], preferred_element_type=F32).astype(BF16)
            for to in range(experts):
                xs[side, to, m] = put[to * cap : (to + 1) * cap]
        for k in range(1, experts):
            x_copy(side, (e + k) % experts).start()
        xr[side, e] = xs[side, e]

    def x_landed(side):
        arrive(xr.at[side, pl.ds(1, experts - 1)], x_sem.at[1, side])

    assign(0, routes_ref)
    dispatch(0, tok_own)
    near_mate.start()
    own_in.start()

    counted = jnp.zeros((8, experts), F32)
    summed = jnp.zeros((8, experts), F32)
    present = jnp.zeros((8, 1), F32)
    for m in range(micro):
        logits = lax.dot_general(
            router_ref[...], tok_own[m], (((1,), (1,)), ((), ())), preferred_element_type=F32
        )
        row = routes_ref[m : m + 1, :]
        hot = jnp.where(lax.broadcasted_iota(jnp.int32, (experts, tok), 0) == row, 1.0, 0.0)
        chosen = jnp.sum(logits * hot, axis=0, keepdims=True)
        gate[m] = spread(1.0 / (1.0 + jnp.exp(-chosen)))
        exps = jnp.exp(logits)
        probs = exps / jnp.sum(exps, axis=0, keepdims=True)
        modal = lax.broadcasted_iota(jnp.int32, (8, tok), 0) == modality_ref[m : m + 1, :]
        modal = jnp.where(modal, 1.0, 0.0)
        counted += lax.dot_general(
            modal, hot, (((1,), (1,)), ((), ())),
            precision=lax.Precision.HIGHEST, preferred_element_type=F32,
        )
        summed += lax.dot_general(
            modal, probs, (((1,), (1,)), ((), ())),
            precision=lax.Precision.HIGHEST, preferred_element_type=F32,
        )
        present += jnp.sum(modal, axis=1, keepdims=True)
    sums[0] = jnp.zeros((8, 128), F32)
    sums[0, 0:2, 0:experts] = counted[0:2]
    sums[0, 2:4, 0:experts] = summed[0:2]
    sums[0, 4:6, 0:experts] = jnp.broadcast_to(present[0:2], (2, experts))

    def tell_e(k, carry):
        remote(
            sums.at[0], stats_e.at[e], stat_sem.at[0, 0], stat_sem.at[1, 0], expert=(e + k) % experts
        ).start()
        return carry

    def tell_d(k, carry):
        remote(
            sums.at[1], stats_d.at[p], stat_sem.at[0, 1], stat_sem.at[1, 1], dp=(p + k) % ranks
        ).start()
        return carry

    lax.fori_loop(1, experts, tell_e, 0)
    for i in range(pieces):
        out_mate[i].start()
        own_out[i].start()
    assign_back(0)

    def second_stats():
        arrive(stats_e.at[pl.ds(1, experts - 1)], stat_sem.at[1, 0])
        stats_e[e] = sums[0]
        sums[1] = jnp.sum(stats_e[...], axis=0)
        lax.fori_loop(1, ranks, tell_d, 0)

    half_w = width // 2

    def first_dot(side, which, at):
        left = xr[side, :, :, :, pl.ds(pl.multiple_of(which * half_w, 128), half_w)]
        right = win[pl.ds(pl.multiple_of(which * half_w, 16), half_w), pl.ds(at, tile)]
        return jnp.dot(left.reshape(side_rows, half_w), right, preferred_element_type=F32)

    def near_side(side):
        def near_tile(i, carry):
            at = pl.multiple_of(i * tile, 128)
            acc[side, :, pl.ds(at, tile)] = first_dot(side, h, at)
            return carry

        lax.fori_loop(0, half_ff // tile, near_tile, 0)

    def far_sides(sides, j):
        at = pl.multiple_of(j * tile, 128)
        for side in range(sides):
            pre = acc[side, :, pl.ds(at, tile)] + first_dot(side, 1 - h, at)
            half = 0.5 * pre
            curve = jnp.tanh(pre * (C1 + C3 * (pre * pre)))
            hid[side, :, pl.ds(at, tile)] = (half + half * curve).astype(BF16)

    def win_span(blocks, at=0, size=half_ff):
        return win.at[pl.ds(0, blocks * in_rows), pl.ds(at, size)]

    def near_arrived():
        for k in range(1, group):
            arrive(win_rows(peer(k)), near_recv.at[(zl + k) % group])
            pass_near(k).start()

    def near_whole():
        arrive(win_span(group + 1), near_whole_recv)

    def far_arrived(t, which, j):
        q = far_rank(t, which, c)
        arrive(win_rows(q, *chunk(j)), far_recv.at[(q // 2) % group, j])
        pass_far(q, j, 0).start()

    def far_direct(which, j):
        q = far_rank(0, which, c)
        arrive(win_rows(q, *chunk(j)), far_recv.at[(q // 2) % group, j])
        for k in range(1, group):
            pass_far(q, j, k).start()
        pass_far(q, j, 0).start()

    def far_whole(j):
        arrive(win_span(group, *chunk(j)), far_whole_recv.at[j])

    def out_arrived(i):
        for k in range(1, group):
            arrive(wout_rows(place(k, c), i), out_recv.at[(zl + k) % group, i])
            pass_out(k, i).start()

    def out_whole(i):
        span = wout.at[pl.ds(0, (group + 1) * out_rows), pl.ds(i * tile_w, tile_w)]
        arrive(span, out_whole_recv.at[i])

    block = side_rows // 2
    block_e = experts // 2

    def second(i, low, high):
        def step(k, carry):
            side, at = low + k // 2, pl.multiple_of((k % 2) * block, 16)
            got = jnp.dot(
                hid[side, pl.ds(at, block), :],
                wout[:, i * tile_w : (i + 1) * tile_w],
                preferred_element_type=F32,
            )
            if i < direct and low == 0:
                near = w_part[i, pl.ds((k % 2) * block_e, block_e)].reshape(block, tile_w)
                got += jnp.where(inner, near.astype(F32), 0.0)
            got = got.astype(BF16).reshape(block_e, micro, cap, tile_w)
            ys[side, i, pl.ds((k % 2) * block_e, block_e)] = got
            return carry

        lax.fori_loop(0, 2 * (high - low), step, 0)

    def w_copy(i):
        return remote(ys.at[2, i], w_part.at[i], w_send, w_recv.at[i], dp=far_in)

    def y_start(side, i):
        for k in range(1, experts):
            to = (e + k) % experts
            remote(
                ys.at[side, i, to], yr.at[side, i, e], y_send.at[side], y_recv.at[side, i], expert=to
            ).start()
        yr[side, i, e] = ys[side, i, e]

    def y_landed(side, i):
        arrive(yr.at[side, i, pl.ds(1, experts - 1)], y_recv.at[side, i])

    def combine(side, i, m):
        back = yr[side, i, :, m].reshape(slots_all, tile_w)
        return jnp.dot(back_hot[side, m], back, preferred_element_type=F32)

    def z_copy(side, i):
        return remote(
            zs.at[side - 1, i], zr.at[i], z_send.at[side - 1], z_recv.at[i],
            dp=far_out if side == 1 else far_in,
        )

    def give_back(side, i):
        y_landed(side, i)
        for m in range(micro):
            zs[side - 1, i, m] = combine(side, i, m).astype(BF16)
        z_copy(side, i).start()

    @pl.when(inner)
    def _():
        for which in range(2):
            arrive(routes_far.at[which], routes_sem.at[which])
            arrive(tok_far.at[which], tok_sem.at[which])
            assign(1 + which, routes_far.at[which])
            dispatch(1 + which, tok_far.at[which])
            assign_back(1 + which)
            if which == 0:
                far_direct(0, 0)
                far_direct(0, 1)
                for i in range(2, early):
                    for copy in out_peers[i]:
                        copy.start()
        second_stats()
        near_arrived()
        x_landed(0)
        near_whole()
        near_side(0)
        x_landed(1)
        near_side(1)
        x_landed(2)
        near_side(2)
        for j in range(2, parts):
            far_direct(0, j)

        def far_next(j):
            far_direct(1, j)
            for t in range(1, pairs):
                far_arrived(t, 0, j)
                far_arrived(t, 1, j)

        far_next(0)

        def far_step(j, carry):
            @pl.when(j < parts - 1)
            def _():
                far_next(j + 1)

            @pl.when(j == parts - 2)
            def _():
                for i in range(early, pieces):
                    for copy in out_peers[i]:
                        copy.start()
                out_arrived(0)

            far_whole(j)
            far_sides(3, j)
            return carry

        lax.fori_loop(0, parts, far_step, 0)

        def own(i):
            if i < direct:
                arrive(w_part.at[i], w_recv.at[i])
            second(i, 0, 1)

        def far_piece(i):
            out_whole(i)
            second(i, 1, 2)
            y_start(1, i)
            second(i, 2, 3)
            if i < direct:
                w_copy(i).start()
            else:
                y_start(2, i)

        out_arrived(1)
        far_piece(0)
        far_piece(1)
        for i in range(2, pieces):
            if i >= pieces - 2:
                give_back(1, i - pieces + 2)
            out_arrived(i)
            if i == pieces - 2:
                own(0)
                y_start(0, 0)
            if i == pieces - 1:
                own(1)
            far_piece(i)
            if i == pieces - 2:
                give_back(2, i - 1)
        y_start(0, 1)
        for i in range(2, pieces):
            own(i)
            y_start(0, i)
        give_back(2, pieces - 2)
        for i in range(2, pieces):
            give_back(1, i)
        give_back(2, pieces - 1)

    @pl.when(outer)
    def _():
        second_stats()
        near_arrived()
        x_landed(0)
        near_whole()
        near_side(0)
        for i in range(early):
            out_arrived(i)

        def far_step(j, carry):
            for t in range(pairs):
                far_arrived(t, 0, j)
                far_arrived(t, 1, j)
            far_whole(j)
            far_sides(1, j)
            return carry

        lax.fori_loop(0, parts, far_step, 0)
        for i in range(pieces):
            if i >= early:
                out_arrived(i)
            out_whole(i)
            second(i, 0, 1)
            y_start(0, i)

    arrive(stats_d.at[pl.ds(1, ranks - 1)], stat_sem.at[1, 1])
    stats_d[p] = sums[1]
    sums[2] = jnp.sum(stats_d[...], axis=0)
    modal_counts = sums[2, 4:6, 0:experts]
    load_ref[0] = experts * sums[2, 0:2, 0:experts] / modal_counts
    load_ref[1] = experts * sums[2, 2:4, 0:experts] / modal_counts

    @pl.when(inner)
    def _():
        for i in range(direct):
            zr[i] = jnp.zeros((micro, tok, tile_w), BF16)

    def result_copy(i):
        part = (slice(None), slice(None), pl.ds(i * tile_w, tile_w))
        return pltpu.make_async_copy(result.at[part], mixed_ref.at[part], result_sem)

    arrive(stats_e.at[pl.ds(1, experts - 1)], stat_sem.at[0, 0])
    arrive(stats_d.at[pl.ds(1, ranks - 1)], stat_sem.at[0, 1])
    tok_copy.wait_send()
    routes_copy.wait_send()
    arrive(win_span(3 * group), in_send.at[0])
    arrive(wout.at[pl.ds(0, (2 * group - 1) * out_rows), :], out_send)
    arrive(xr.at[0, pl.ds(1, experts - 1)], x_sem.at[0, 0])

    @pl.when(inner)
    def _():
        arrive(win_span(2 * (group - 1)), in_send.at[1])
        for side in (1, 2):
            arrive(xr.at[side, pl.ds(1, experts - 1)], x_sem.at[0, side])
        arrive(yr.at[1, :, pl.ds(1, experts - 1)], y_send.at[1])
        arrive(yr.at[2, pl.ds(direct, pieces - direct), pl.ds(1, experts - 1)], y_send.at[2])
        arrive(w_part, w_send)

    for i in range(pieces):
        y_landed(0, i)
        kept = [combine(0, i, m) for m in range(micro)]
        if i < direct:

            @pl.when(outer)
            def _(i=i):
                arrive(zr.at[i], z_recv.at[i])
        else:
            arrive(zr.at[i], z_recv.at[i])
        for m in range(micro):
            both = kept[m] + zr[i, m].astype(F32)
            scale = jnp.concatenate([gate[m]] * (tile_w // tok), axis=1)
            result[m, :, i * tile_w : (i + 1) * tile_w] = (both * scale).astype(BF16)
        result_copy(i).start()

    arrive(yr.at[0, :, pl.ds(1, experts - 1)], y_send.at[0])
    pltpu.make_async_copy(result, mixed_ref, result_sem).wait()

    @pl.when(inner)
    def _():
        arrive(zs.at[0], z_send.at[0])
        arrive(zs.at[1, pl.ds(direct, pieces - direct)], z_send.at[1])


def on_device(tokens, modality, routes, router, w_in, w_out):
    micro, tok, width = tokens.shape
    experts = router.shape[1]
    cap = 2 * tok // experts
    ranks = lax.axis_size("dp")
    group = ranks // 4
    half_ff = w_in.shape[2] // 2
    tile_w = 256 if width % 256 == 0 else 128
    pieces = width // tile_w
    tile = 512 if half_ff % 512 == 0 else 128
    parts = half_ff // tile

    dma = pltpu.SemaphoreType.DMA
    vmem = pl.BlockSpec(memory_space=pltpu.VMEM)
    hbm = pl.BlockSpec(memory_space=pl.ANY)
    rows = experts * micro * cap
    mixed, load = pl.pallas_call(
        functools.partial(layer_kernel, experts, ranks, tile),
        out_shape=(
            jax.ShapeDtypeStruct(tokens.shape, BF16),
            jax.ShapeDtypeStruct((2, 2, experts), F32),
        ),
        in_specs=[hbm] + [vmem] * 3 + [hbm] * 2,
        out_specs=(hbm, vmem),
        scratch_shapes=[
            pltpu.VMEM((micro, tok, width), BF16),
            pltpu.VMEM((micro, tok, width), BF16),
            pltpu.VMEM((2, micro, tok, width), BF16),
            pltpu.VMEM((2, micro, tok), jnp.int32),
            pltpu.VMEM((3, micro, 8, tok), F32),
            pltpu.VMEM((3, micro, tok, experts * cap), BF16),
            pltpu.VMEM((micro, tok, tok), F32),
            pltpu.VMEM((3, 8, 128), F32),
            pltpu.VMEM((experts, 8, 128), F32),
            pltpu.VMEM((ranks, 8, 128), F32),
            pltpu.VMEM((width, half_ff), BF16),
            pltpu.VMEM((half_ff, width), BF16),
            pltpu.VMEM((3, experts, micro, cap, width), BF16),
            pltpu.VMEM((3, experts, micro, cap, width), BF16),
            pltpu.VMEM((3, rows, half_ff), F32),
            pltpu.VMEM((3, rows, half_ff), BF16),
            pltpu.VMEM((3, pieces, experts, micro, cap, tile_w), BF16),
            pltpu.VMEM((3, pieces, experts, micro, cap, tile_w), BF16),
            pltpu.VMEM((2, pieces, micro, tok, tile_w), BF16),
            pltpu.VMEM((pieces, micro, tok, tile_w), BF16),
            pltpu.VMEM((2, experts, micro, cap, tile_w), BF16),
            dma((3,)),
            dma((3,)),
            dma((2, 2)),
            dma((2,)),
            dma((group,)),
            dma,
            dma((group, parts)),
            dma((parts,)),
            dma,
            dma((group, pieces)),
            dma((pieces,)),
            dma((2, 3)),
            dma((3,)),
            dma((3, pieces)),
            dma((2,)),
            dma((pieces,)),
            dma,
            dma((2,)),
            dma,
            dma,
        ],
        compiler_params=pltpu.CompilerParams(
            collective_id=0, has_side_effects=True, vmem_limit_bytes=64 * 1024 * 1024 - 65536
        ),
    )(tokens, routes[:, :, 0], modality, router.T, w_in[0], w_out[0])
    return (mixed, load)


def solution(mesh):
    placed = (
        P(None, ("expert", "dp"), None),
        P(None, ("expert", "dp")),
        P(None, ("expert", "dp"), None),
        P(),
        P("expert", "dp", None),
        P("expert", "dp", None),
    )
    return jax.shard_map(
        on_device,
        mesh=mesh,
        in_specs=placed,
        out_specs=(P(None, ("expert", "dp"), None), P()),
        check_vma=False,
    )
```

time: 135 us -> 121 us (0.90)
  Pallas kernels: 130 us -> 117 us
    pallas_call x1, Pallas kernels: 130 us -> 117 us  [on_device(): pl.pallas_call(functools.partial(layer_kernel, experts, ranks, tile), out...]
where the time goes in v2:
time: 121 us
  Pallas kernels  117 us (97%)
  local copies, waits for them, and re-layouts  3.21 us (3%)
    pallas_call x1, Pallas kernels, on_device(): pl.pallas_call(functools.partial(layer_kernel, experts, ranks, tile), out...  117 us
    unnamed x2, local copies, waits for them, and re-layouts  3.21 us

profile of v2, /device:TPU:0, one launch (start us, length us, event | category | flops | bytes accessed | tf_op | source)
XLA Modules:
  0.0 120.7 jit_solution(4468775737447735598)
XLA Ops:
  0.6 116.9 %shard_map.77 = (bf16[2,128,1280]{2,1,0:T(8,128)(2,1)}, f32[2,2,4]{2,1,0:T(2,128)}) custom-call(bf16[2,128,1280]{2,1,0:T(8,128)(2,1)} %tokens_ref.1, s32[2,128]{1,0:T(2,128)} %bitcast.7, s32[2,128]{1,0:T(2,128)} %modality_ref.1, bf16[4,1280]{1,0:T(4,128)(2,1)} %bitcast.6, bf16[160,5120]{1,0:T(8,128)(2,1)} %bitcast.4, bf16[640,1280]{1,0:T(8,128)(2,1)} %bitcast.5), custom_call_target="tpu_custom_call" | custom-call | tf_op jit(solution)/shard_map/pallas_call | solution.py:645
  117.5 2.0 %copy.10 = bf16[2,128,1280]{2,1,0:T(8,128)(2,1)} copy(bf16[2,128,1280]{2,1,0:T(8,128)(2,1)} %get-tuple-element.4) | data formatting | bytes 1310720
  119.5 1.2 %copy.11 = f32[2,2,4]{2,1,0:T(2,128)} copy(f32[2,2,4]{2,1,0:T(2,128)} %get-tuple-element.5) | data formatting | bytes 128

commit v3 on v2

--- a/solution.py
+++ b/solution.py
@@ -19,6 +19,7 @@
     experts,
     ranks,
     tile,
+    far_tile,
     tokens_ref,
     routes_ref,
     modality_ref,
@@ -28,7 +29,6 @@
     mixed_ref,
     load_ref,
     tok_own,
-    result,
     tok_far,
     routes_far,
     slot_row,
@@ -67,7 +67,6 @@
     w_send,
     w_recv,
     load_sem,
-    result_sem,
 ):
     micro, tok, width = tokens_ref.shape
     in_rows, ff = w_in_ref.shape
@@ -134,10 +133,12 @@
     def arrive(ref, sem):
         pltpu.make_async_copy(ref, ref, sem).wait()
 
-    parts = half_ff // tile
+    parts = half_ff // far_tile
+    ahead_parts = parts * 2 // 5
 
     def chunk(j):
-        return (j * tile if isinstance(j, int) else pl.multiple_of(j * tile, 128), tile)
+        at = j * far_tile
+        return (at if isinstance(j, int) else pl.multiple_of(at, 128), far_tile)
 
     def win_rows(q, start=0, size=half_ff):
         return win.at[pl.ds(pl.multiple_of(q * in_rows, 16), in_rows), pl.ds(start, size)]
@@ -211,7 +212,7 @@
     tok_load.wait()
     pl.semaphore_wait(barrier, experts + ranks - 2)
 
-    early = pieces - 1
+    early = pieces - 2
     routes_copy.start()
     tok_copy.start()
 
@@ -227,11 +228,11 @@
 
     @pl.when(outer)
     def _():
-        for copy in far_copies[:2]:
+        for copy in far_copies[:ahead_parts]:
             copy.start()
         for copy in near_peers:
             copy.start()
-        for copy in far_copies[2:]:
+        for copy in far_copies[ahead_parts:]:
             copy.start()
         for i in range(pieces):
             for copy in out_peers[i]:
@@ -345,7 +346,7 @@
 
     half_w = width // 2
 
-    def first_dot(side, which, at):
+    def first_dot(side, which, at, tile):
         left = xr[side, :, :, :, pl.ds(pl.multiple_of(which * half_w, 128), half_w)]
         right = win[pl.ds(pl.multiple_of(which * half_w, 16), half_w), pl.ds(at, tile)]
         return jnp.dot(left.reshape(side_rows, half_w), right, preferred_element_type=F32)
@@ -353,18 +354,22 @@
     def near_side(side):
         def near_tile(i, carry):
             at = pl.multiple_of(i * tile, 128)
-            acc[side, :, pl.ds(at, tile)] = first_dot(side, h, at)
+            acc[side, :, pl.ds(at, tile)] = first_dot(side, h, at, tile)
             return carry
 
         lax.fori_loop(0, half_ff // tile, near_tile, 0)
 
     def far_sides(sides, j):
-        at = pl.multiple_of(j * tile, 128)
+        at = pl.multiple_of(j * far_tile, 128)
         for side in range(sides):
-            pre = acc[side, :, pl.ds(at, tile)] + first_dot(side, 1 - h, at)
+            if side == 2:
+                left = xr[side].reshape(side_rows, width)
+                pre = jnp.dot(left, win[:, pl.ds(at, far_tile)], preferred_element_type=F32)
+            else:
+                pre = acc[side, :, pl.ds(at, far_tile)] + first_dot(side, 1 - h, at, far_tile)
             half = 0.5 * pre
             curve = jnp.tanh(pre * (C1 + C3 * (pre * pre)))
-            hid[side, :, pl.ds(at, tile)] = (half + half * curve).astype(BF16)
+            hid[side, :, pl.ds(at, far_tile)] = (half + half * curve).astype(BF16)
 
     def win_span(blocks, at=0, size=half_ff):
         return win.at[pl.ds(0, blocks * in_rows), pl.ds(at, size)]
@@ -460,8 +465,8 @@
             dispatch(1 + which, tok_far.at[which])
             assign_back(1 + which)
             if which == 0:
-                far_direct(0, 0)
-                far_direct(0, 1)
+                for j in range(ahead_parts):
+                    far_direct(0, j)
                 for i in range(2, early):
                     for copy in out_peers[i]:
                         copy.start()
@@ -470,11 +475,11 @@
         x_landed(0)
         near_whole()
         near_side(0)
+        for j in range(ahead_parts, ahead_parts + 2):
+            far_direct(0, j)
         x_landed(1)
         near_side(1)
-        x_landed(2)
-        near_side(2)
-        for j in range(2, parts):
+        for j in range(ahead_parts + 2, parts):
             far_direct(0, j)
 
         def far_next(j):
@@ -484,6 +489,7 @@
                 far_arrived(t, 1, j)
 
         far_next(0)
+        x_landed(2)
 
         def far_step(j, carry):
             @pl.when(j < parts - 1)
@@ -522,24 +528,25 @@
         far_piece(0)
         far_piece(1)
         for i in range(2, pieces):
-            if i >= pieces - 2:
-                give_back(1, i - pieces + 2)
+            if i == pieces - 1:
+                give_back(2, pieces - 3)
             out_arrived(i)
             if i == pieces - 2:
                 own(0)
                 y_start(0, 0)
             if i == pieces - 1:
+                give_back(1, 0)
                 own(1)
             far_piece(i)
-            if i == pieces - 2:
-                give_back(2, i - 1)
         y_start(0, 1)
         for i in range(2, pieces):
             own(i)
             y_start(0, i)
-        give_back(2, pieces - 2)
-        for i in range(2, pieces):
-            give_back(1, i)
+            if i == pieces - 3:
+                give_back(2, pieces - 2)
+        for back in range(1, pieces - 1):
+            give_back(1, back)
+        give_back(1, pieces - 1)
         give_back(2, pieces - 1)
 
     @pl.when(outer)
@@ -580,10 +587,6 @@
         for i in range(direct):
             zr[i] = jnp.zeros((micro, tok, tile_w), BF16)
 
-    def result_copy(i):
-        part = (slice(None), slice(None), pl.ds(i * tile_w, tile_w))
-        return pltpu.make_async_copy(result.at[part], mixed_ref.at[part], result_sem)
-
     arrive(stats_e.at[pl.ds(1, experts - 1)], stat_sem.at[0, 0])
     arrive(stats_d.at[pl.ds(1, ranks - 1)], stat_sem.at[0, 1])
     tok_copy.wait_send()
@@ -614,11 +617,9 @@
         for m in range(micro):
             both = kept[m] + zr[i, m].astype(F32)
             scale = jnp.concatenate([gate[m]] * (tile_w // tok), axis=1)
-            result[m, :, i * tile_w : (i + 1) * tile_w] = (both * scale).astype(BF16)
-        result_copy(i).start()
+            mixed_ref[m, :, i * tile_w : (i + 1) * tile_w] = (both * scale).astype(BF16)
 
     arrive(yr.at[0, :, pl.ds(1, experts - 1)], y_send.at[0])
-    pltpu.make_async_copy(result, mixed_ref, result_sem).wait()
 
     @pl.when(inner)
     def _():
@@ -636,22 +637,22 @@
     tile_w = 256 if width % 256 == 0 else 128
     pieces = width // tile_w
     tile = 512 if half_ff % 512 == 0 else 128
-    parts = half_ff // tile
+    far_tile = 256 if half_ff % 256 == 0 else 128
+    parts = half_ff // far_tile
 
     dma = pltpu.SemaphoreType.DMA
     vmem = pl.BlockSpec(memory_space=pltpu.VMEM)
     hbm = pl.BlockSpec(memory_space=pl.ANY)
     rows = experts * micro * cap
     mixed, load = pl.pallas_call(
-        functools.partial(layer_kernel, experts, ranks, tile),
+        functools.partial(layer_kernel, experts, ranks, tile, far_tile),
         out_shape=(
-            jax.ShapeDtypeStruct(tokens.shape, BF16),
-            jax.ShapeDtypeStruct((2, 2, experts), F32),
+            pltpu.VMEM(tokens.shape, BF16),
+            pltpu.VMEM((2, 2, experts), F32),
         ),
         in_specs=[hbm] + [vmem] * 3 + [hbm] * 2,
-        out_specs=(hbm, vmem),
+        out_specs=(vmem, vmem),
         scratch_shapes=[
-            pltpu.VMEM((micro, tok, width), BF16),
             pltpu.VMEM((micro, tok, width), BF16),
             pltpu.VMEM((2, micro, tok, width), BF16),
             pltpu.VMEM((2, micro, tok), jnp.int32),
@@ -665,7 +666,7 @@
             pltpu.VMEM((half_ff, width), BF16),
             pltpu.VMEM((3, experts, micro, cap, width), BF16),
             pltpu.VMEM((3, experts, micro, cap, width), BF16),
-            pltpu.VMEM((3, rows, half_ff), F32),
+            pltpu.VMEM((2, rows, half_ff), F32),
             pltpu.VMEM((3, rows, half_ff), BF16),
             pltpu.VMEM((3, pieces, experts, micro, cap, tile_w), BF16),
             pltpu.VMEM((3, pieces, experts, micro, cap, tile_w), BF16),
@@ -691,10 +692,9 @@
             dma,
             dma((2,)),
             dma,
-            dma,
         ],
         compiler_params=pltpu.CompilerParams(
-            collective_id=0, has_side_effects=True, vmem_limit_bytes=64 * 1024 * 1024 - 65536
+            collective_id=0, has_side_effects=True, vmem_limit_bytes=62 * 1024 * 1024
         ),
     )(tokens, routes[:, :, 0], modality, router.T, w_in[0], w_out[0])
     return (mixed, load)

time: 121 us -> 118 us (0.975)
  Pallas kernels: 117 us -> 115 us
  local copies, waits for them, and re-layouts: 3.21 us -> 1.42 us
    unnamed x2, local copies, waits for them, and re-layouts: 3.21 us -> 1.42 us
    pallas_call x1, Pallas kernels: 117 us -> 115 us  [on_device(): pl.pallas_call(functools.partial(layer_kernel, experts, ranks, tile, far_...]
where the time goes in v3:
time: 118 us; the launch traced here: 117 us
  Pallas kernels  115 us (97%)
  local copies, waits for them, and re-layouts  1.42 us (1%)
    pallas_call x1, Pallas kernels, on_device(): pl.pallas_call(functools.partial(layer_kernel, experts, ranks, tile, far_...  115 us

profile of v3, /device:TPU:0, one launch (start us, length us, event | category | flops | bytes accessed | tf_op | source)
XLA Modules:
  0.0 117.4 jit_solution(8809396914174732099)
XLA Ops:
  0.6 115.3 %shard_map.77 = (bf16[2,128,1280]{2,1,0:T(8,128)(2,1)S(1)}, f32[2,2,4]{2,1,0:T(2,128)S(1)}) custom-call(bf16[2,128,1280]{2,1,0:T(8,128)(2,1)} %tokens_ref.1, s32[2,128]{1,0:T(2,128)} %bitcast.7, s32[2,128]{1,0:T(2,128)} %modality_ref.1, bf16[4,1280]{1,0:T(4,128)(2,1)} %bitcast.6, bf16[160,5120]{1,0:T(8,128)(2,1)} %bitcast.4, bf16[640,1280]{1,0:T(8,128)(2,1)} %bitcast.5), custom_call_target="tpu_custom_call" | custom-call | tf_op jit(solution)/shard_map/pallas_call | solution.py:647
  116.0 0.8 copy.10
  116.8 0.6 copy.11

commit v4 on v3

--- a/solution.py
+++ b/solution.py
@@ -528,24 +528,26 @@
         far_piece(0)
         far_piece(1)
         for i in range(2, pieces):
-            if i == pieces - 1:
-                give_back(2, pieces - 3)
-            out_arrived(i)
             if i == pieces - 2:
                 own(0)
                 y_start(0, 0)
             if i == pieces - 1:
+                give_back(2, pieces - 3)
+                own(1)
+                y_start(0, 1)
+            out_arrived(i)
+            if i == pieces - 1:
                 give_back(1, 0)
-                own(1)
             far_piece(i)
-        y_start(0, 1)
+        for back in range(1, pieces - 2):
+            give_back(1, back)
         for i in range(2, pieces):
             own(i)
             y_start(0, i)
             if i == pieces - 3:
                 give_back(2, pieces - 2)
-        for back in range(1, pieces - 1):
-            give_back(1, back)
+            if i == pieces - 2:
+                give_back(1, pieces - 2)
         give_back(1, pieces - 1)
         give_back(2, pieces - 1)
 

time: 118 us -> 116 us (0.983)
  Pallas kernels: 115 us -> 113 us
    pallas_call x1, Pallas kernels: 115 us -> 113 us  [on_device(): pl.pallas_call(functools.partial(layer_kernel, experts, ranks, tile, far_...]
where the time goes in v4:
time: 116 us; the launch traced here: 115 us
  Pallas kernels  113 us (97%)
  local copies, waits for them, and re-layouts  1.42 us (1%)
    pallas_call x1, Pallas kernels, on_device(): pl.pallas_call(functools.partial(layer_kernel, experts, ranks, tile, far_...  113 us

profile of v4, /device:TPU:0, one launch (start us, length us, event | category | flops | bytes accessed | tf_op | source)
XLA Modules:
  0.0 114.8 jit_solution(16739907414087773863)
XLA Ops:
  0.6 112.7 %shard_map.77 = (bf16[2,128,1280]{2,1,0:T(8,128)(2,1)S(1)}, f32[2,2,4]{2,1,0:T(2,128)S(1)}) custom-call(bf16[2,128,1280]{2,1,0:T(8,128)(2,1)} %tokens_ref.1, s32[2,128]{1,0:T(2,128)} %bitcast.7, s32[2,128]{1,0:T(2,128)} %modality_ref.1, bf16[4,1280]{1,0:T(4,128)(2,1)} %bitcast.6, bf16[160,5120]{1,0:T(8,128)(2,1)} %bitcast.4, bf16[640,1280]{1,0:T(8,128)(2,1)} %bitcast.5), custom_call_target="tpu_custom_call" | custom-call | tf_op jit(solution)/shard_map/pallas_call | solution.py:649
  113.4 0.8 copy.10
  114.2 0.6 copy.11
